TPU v7x, 32 devices: a 4x4x1 block of a 4x4x8 slice. The times are simulated.
32 devices in a mesh: grp: 1 (over z), dz: 4 (over y), dy: 4 (over x), dx: 2 (over core).
Axes of the slice: x: 4, y: 4, z: 1, core: 2. Of those that a mesh axis runs over, the one named last changes fastest.
The devices are a block of a 4x4x8 slice.
Arguments:
- x_in: bfloat16 [6144, 7168], P(('grp', 'dx', 'dz'), 'dy')
- w_gate: bfloat16 [7168, 20480], P('dy', ('dz', 'dx'))
- w_up: bfloat16 [7168, 20480], P('dy', ('dz', 'dx'))
- w_down: bfloat16 [20480, 7168], P('dz', ('dy', 'dx'))
Outputs:
- output: bfloat16 [6144, 7168], P(('grp', 'dx', 'dz'), 'dy')
All inputs are finite; a program needn't handle non-finite values.
Results may differ from a plain program's by a relative error of at most 0.0124762.
Values are sent between devices in bfloat16 or wider.
A program may use at most 768 MiB of HBM per device.

v0:
```python
import jax
import jax.numpy as jnp
from jax import lax
from jax.sharding import PartitionSpec as P


def solution(mesh):
    x_spec = P(("grp", "dx", "dz"), "dy")
    w_in_spec = P("dy", ("dz", "dx"))
    w_out_spec = P("dz", ("dy", "dx"))

    def local_mlp(x_blk, wg_blk, wu_blk, wd_blk):
        x_rows = lax.all_gather(x_blk, "dz", axis=0, tiled=True)
        wg_cols = lax.all_gather(wg_blk, "dx", axis=1, tiled=True)
        wu_cols = lax.all_gather(wu_blk, "dx", axis=1, tiled=True)
        gate_part = jnp.dot(x_rows, wg_cols, preferred_element_type=jnp.float32)
        up_part = jnp.dot(x_rows, wu_cols, preferred_element_type=jnp.float32)
        gate_sum = lax.psum_scatter(gate_part, "dy", scatter_dimension=0, tiled=True)
        up_sum = lax.psum_scatter(up_part, "dy", scatter_dimension=0, tiled=True)
        gate_val = gate_sum.astype(jnp.bfloat16).astype(jnp.float32)
        up_val = up_sum.astype(jnp.bfloat16).astype(jnp.float32)
        hidden = (jax.nn.silu(gate_val) * up_val).astype(jnp.bfloat16)
        h_rows = lax.all_gather(hidden, "dy", axis=0, tiled=True)
        wd_cols = lax.all_gather(wd_blk, "dx", axis=1, tiled=True)
        out_part = jnp.dot(h_rows, wd_cols, preferred_element_type=jnp.float32)
        out_sum = lax.psum_scatter(out_part, "dz", scatter_dimension=0, tiled=True)
        return out_sum.astype(jnp.bfloat16)

    return jax.shard_map(local_mlp, mesh=mesh, in_specs=(x_spec, w_in_spec, w_in_spec, w_out_spec), out_specs=x_spec, check_vma=False)
```

profile of v0, /device:TPU:97, one launch (start us, length us, event | category | flops | bytes accessed | tf_op | source)
XLA Modules:
  0.0 1834.8 jit_solution(2979737126131833457)
XLA Ops:
  6.6 0.7 all-gather.6.cloned.1.call-update
  7.3 0.1 all-gather.8.cloned.1.call-start
  7.4 0.7 all-gather.8.cloned.1.call-update
  8.1 0.1 all-gather.10.cloned.1.call-start
  8.2 0.7 all-gather.10.cloned.1.call-update
  8.9 0.1 reduce-scatter.4.cloned.1.call-start
  9.0 106.8 %all-gather.6.cloned.1.call-done = bf16[3072,1792]{1,0:T(8,128)(2,1)} async-done(((bf16[768,1792]{1,0:T(8,128)(2,1)}), bf16[3072,1792]{1,0:T(8,128)(2,1)}) %all-gather.6.cloned.1.call-update) | async-done | bytes 11010064 | tf_op jit(solution)/shard_map/all_gather | solution.py:13
  115.8 36.8 %all-gather.8.cloned.1.call-done = bf16[1792,5120]{1,0:T(8,128)(2,1)} async-done(((bf16[1792,2560]{1,0:T(8,128)(2,1)}), bf16[1792,5120]{1,0:T(8,128)(2,1)}) %all-gather.8.cloned.1.call-update) | async-done | bytes 18350096 | tf_op jit(solution)/shard_map/all_gather | solution.py:14
  152.5 66.4 %fusion.5 = f32[3072,5120]{1,0:T(8,128)} fusion(bf16[3072,1792]{1,0:T(8,128)(2,1)} %all-gather.6.cloned.1.call-done, bf16[1792,5120]{1,0:T(8,128)(2,1)} %all-gather.8.cloned.1.call-done), kind=kOutput, calls=%fused_computation.7 | convolution fusion | flops 56371445760 | bytes 92274688 | tf_op jit(solution)/shard_map/dot_general | solution.py:16
  218.9 0.1 reduce-scatter.4.cloned.1.call-update
  219.0 0.1 reduce-scatter.6.cloned.1.call-start
  219.1 66.5 %fusion.6 = f32[3072,5120]{1,0:T(8,128)} fusion(bf16[3072,1792]{1,0:T(8,128)(2,1)} %all-gather.6.cloned.1.call-done, bf16[1792,5120]{1,0:T(8,128)(2,1)} %all-gather.10.cloned.1.call-done), kind=kOutput, calls=%fused_computation.8 | convolution fusion | flops 56371445760 | bytes 92274688 | tf_op jit(solution)/shard_map/dot_general | solution.py:17
  285.6 0.1 all-gather.14.cloned.1.call-start
  285.7 0.6 all-gather.14.cloned.1.call-update
  286.3 0.1 all-gather.12.cloned.1.call-start
  286.3 450.4 %reduce-scatter.4.cloned.1.call-done = f32[768,5120]{1,0:T(8,128)} async-done(((f32[3072,5120]{1,0:T(8,128)}), f32[768,5120]{1,0:T(8,128)}) %reduce-scatter.4.cloned.1.call-update) | async-done | bytes 15728656 | tf_op jit(solution)/shard_map/reduce_scatter | solution.py:18
  736.7 518.6 %reduce-scatter.6.cloned.1.call-done = f32[768,5120]{1,0:T(8,128)} async-done(((f32[3072,5120]{1,0:T(8,128)}), f32[768,5120]{1,0:T(8,128)}) %reduce-scatter.6.cloned.1.call-update) | async-done | bytes 15728656 | tf_op jit(solution)/shard_map/reduce_scatter | solution.py:19
  1255.3 13.9 fusion.4
  1269.4 0.2 reduce-scatter.8.cloned.1.call-start
  1269.6 21.1 %all-gather.14.cloned.1.call-done = bf16[5120,1792]{1,0:T(8,128)(2,1)} async-done(((bf16[5120,896]{1,0:T(8,128)(2,1)}), bf16[5120,1792]{1,0:T(8,128)(2,1)}) %all-gather.14.cloned.1.call-update) | async-done | bytes 18350096 | tf_op jit(solution)/shard_map/all_gather | solution.py:24
  1290.7 276.6 %all-gather.12.cloned.1.call-done = bf16[3072,5120]{1,0:T(8,128)(2,1)} async-done(((bf16[768,5120]{1,0:T(8,128)(2,1)}), bf16[3072,5120]{1,0:T(8,128)(2,1)}) %all-gather.12.cloned.1.call-update) | async-done | bytes 31457296 | tf_op jit(solution)/shard_map/all_gather | solution.py:23
  1567.3 67.3 %fusion.7 = f32[3072,1792]{1,0:T(8,128)} fusion(bf16[3072,5120]{1,0:T(8,128)(2,1)} %all-gather.12.cloned.1.call-done, bf16[5120,1792]{1,0:T(8,128)(2,1)} %all-gather.14.cloned.1.call-done), kind=kOutput, calls=%fused_computation.9 | convolution fusion | flops 56371445760 | bytes 71827456 | tf_op jit(solution)/shard_map/dot_general | solution.py:25
  1634.7 188.9 %reduce-scatter.8.cloned.1.call-done = f32[768,1792]{1,0:T(8,128)} async-done(((f32[3072,1792]{1,0:T(8,128)}), f32[768,1792]{1,0:T(8,128)}) %reduce-scatter.8.cloned.1.call-update) | async-done | bytes 5505040 | tf_op jit(solution)/shard_map/reduce_scatter | solution.py:26
  1823.6 4.4 convert_element_type.23
  (5 shorter events, 0.2 us)
Async XLA Ops:
  6.5 109.2 %all-gather.6.cloned.1.call-start = ((), (), s32[]{:S(2)}) async-start(), calls=%async_computation.3 | async-start | bytes 13762560 | tf_op jit(solution)/shard_map/all_gather | solution.py:13
  7.3 145.2 %all-gather.8.cloned.1.call-start = ((), (), s32[]{:S(2)}) async-start(), calls=%async_computation.4 | async-start | bytes 27525120 | tf_op jit(solution)/shard_map/all_gather | solution.py:14
  8.1 211.0 %all-gather.10.cloned.1.call-start = ((), (), s32[]{:S(2)}) async-start(), calls=%async_computation.6 | async-start | bytes 27525120 | tf_op jit(solution)/shard_map/all_gather | solution.py:15
  8.9 727.8 %reduce-scatter.4.cloned.1.call-start = ((), (), s32[]{:S(2)}) async-start(), calls=%async_computation.5 | async-start | bytes 78643200 | tf_op jit(solution)/shard_map/reduce_scatter | solution.py:18
  219.0 1036.3 %reduce-scatter.6.cloned.1.call-start = ((), (), s32[]{:S(2)}) async-start(), calls=%async_computation.7 | async-start | bytes 78643200 | tf_op jit(solution)/shard_map/reduce_scatter | solution.py:19
  285.6 1005.1 %all-gather.14.cloned.1.call-start = ((), (), s32[]{:S(2)}) async-start(), calls=%async_computation.9 | async-start | bytes 27525120 | tf_op jit(solution)/shard_map/all_gather | solution.py:24
  286.3 1281.0 %all-gather.12.cloned.1.call-start = ((), (), s32[]{:S(2)}) async-start(), calls=%async_computation.8 | async-start | bytes 39321600 | tf_op jit(solution)/shard_map/all_gather | solution.py:23
  1269.4 554.2 %reduce-scatter.8.cloned.1.call-start = ((), (), s32[]{:S(2)}) async-start(), calls=%async_computation.10 | async-start | bytes 27525120 | tf_op jit(solution)/shard_map/reduce_scatter | solution.py:26
Sparse Core Ops, SparseCore 0:
  8.9 106.7 all-gather.5
  117.3 35.1 all-gather.7
  154.1 35.0 all-gather.9
  219.1 517.5 reduce-scatter.3
  738.9 516.3 reduce-scatter.5
  1256.8 33.9 all-gather.13
  1292.3 274.9 all-gather.11
  1634.8 188.7 reduce-scatter.7
where the time goes:
time: 1830 us
  waiting for transfers between devices  1600 us (87%)
  matrix products  200 us (11%)
  other arithmetic  18.3 us (1%)
    reduce_scatter x1, waiting for transfers between devices, local_mlp(): up_sum = lax.psum_scatter(up_part, 'dy', scatter_dimension=0, tiled=True)  519 us
    reduce_scatter x1, waiting for transfers between devices, local_mlp(): lax.psum_scatter(gate_part, 'dy', scatter_dimension=0, tiled=True)  450 us
    all_gather x1, waiting for transfers between devices, local_mlp(): h_rows = lax.all_gather(hidden, 'dy', axis=0, tiled=True)  277 us
    reduce_scatter x1, waiting for transfers between devices, local_mlp(): out_sum = lax.psum_scatter(out_part, 'dz', scatter_dimension=0, tiled=True)  189 us
    all_gather x1, waiting for transfers between devices, local_mlp(): x_rows = lax.all_gather(x_blk, 'dz', axis=0, tiled=True)  107 us
    dot_general x1, matrix products, local_mlp(): out_part = jnp.dot(h_rows, wd_cols, preferred_element_type=jnp.float32)  67.3 us
    dot_general x1, matrix products, local_mlp(): up_part = jnp.dot(x_rows, wu_cols, preferred_element_type=jnp.float32)  66.5 us
    dot_general x1, matrix products, local_mlp(): gate_part = jnp.dot(x_rows, wg_cols, preferred_element_type=jnp.float32)  66.4 us
  transfers between devices with their start and end apart: 8, of which 7 were waited for; matrix products, arithmetic and copies ran while one was open for 8% of the time, Pallas kernels for 0%

commit v1 on v0

v1 whole, which is shorter than its diff:
```python
import jax
import jax.numpy as jnp
from jax import lax
from jax.sharding import PartitionSpec as P


def solution(mesh):
    x_spec = P(("grp", "dx", "dz"), "dy")
    w_in_spec = P("dy", ("dz", "dx"))
    w_out_spec = P("dz", ("dy", "dx"))

    def local_mlp(x_blk, wg_blk, wu_blk, wd_blk):
        wg = lax.all_to_all(wg_blk, "dy", split_axis=1, concat_axis=0, tiled=True)
        wu = lax.all_to_all(wu_blk, "dy", split_axis=1, concat_axis=0, tiled=True)
        wg = lax.all_gather(wg, "dx", axis=1, tiled=True)
        wu = lax.all_gather(wu, "dx", axis=1, tiled=True)
        x_full = lax.all_gather(x_blk, "dy", axis=1, tiled=True)
        x_rows = lax.all_gather(x_full, "dz", axis=0, tiled=True)
        gate = jnp.dot(x_rows, wg, preferred_element_type=jnp.float32)
        up = jnp.dot(x_rows, wu, preferred_element_type=jnp.float32)
        gate = gate.astype(jnp.bfloat16).astype(jnp.float32)
        up = up.astype(jnp.bfloat16).astype(jnp.float32)
        hidden = (jax.nn.silu(gate) * up).astype(jnp.bfloat16)
        n_dy, half = mesh.shape["dy"], wd_blk.shape[0] // mesh.shape["dx"]
        h_rows = lax.all_gather(hidden, "dy", axis=1, tiled=True)
        wd_cols = lax.all_gather(wd_blk, "dx", axis=1, tiled=True)
        sub = half // n_dy
        wd_perm = wd_cols.reshape(mesh.shape["dx"], n_dy, sub, -1).transpose(1, 0, 2, 3).reshape(wd_cols.shape)
        out_part = jnp.dot(h_rows, wd_perm, preferred_element_type=jnp.float32)
        out_sum = lax.psum_scatter(out_part, "dz", scatter_dimension=0, tiled=True)
        return out_sum.astype(jnp.bfloat16)

    return jax.shard_map(local_mlp, mesh=mesh, in_specs=(x_spec, w_in_spec, w_in_spec, w_out_spec), out_specs=x_spec, check_vma=False)
```

time: 1830 us -> 1320 us (0.72)
  waiting for transfers between devices: 1600 us -> 731 us
  blocking collectives: 0 us -> 302 us
  local copies, waits for them, and re-layouts: 0 us -> 67.5 us
    reduce_scatter x2 -> x0, waiting for transfers between devices: 969 us -> none  [the longest x1 519 us: local_mlp(): up_sum = lax.psum_scatter(up_part, 'dy', scatter_dimension=0, tiled=True)]
    all_to_all x0 -> x2, blocking collectives: none -> 302 us  [the longest x1 193 us: local_mlp(): wg = lax.all_to_all(wg_blk, 'dy', split_axis=1, concat_axis=0, tiled=True)]
    all_gather x4 -> x5, waiting for transfers between devices: 420 us -> 539 us  [the longest x1 281 us: local_mlp(): x_rows = lax.all_gather(x_full, 'dz', axis=0, tiled=True)]
    unnamed x0 -> x2, local copies, waits for them, and re-layouts: none -> 25.6 us
    all_to_all x0 -> x2, local copies, waits for them, and re-layouts: none -> 25.6 us  [the longest x1 12.8 us: local_mlp(): wu = lax.all_to_all(wu_blk, 'dy', split_axis=1, concat_axis=0, tiled=True)]
    all_gather x1, waiting for transfers between devices: 21.1 us -> 0.02 us  [local_mlp(): wd_cols = lax.all_gather(wd_blk, 'dx', axis=1, tiled=True)]
  transfers between devices with their start and end apart: 8 -> 7, of which waited for: 7 -> 3; matrix products, arithmetic and copies ran while one was open for 8% -> 15% of each run, Pallas kernels for 0% -> 0%
where the time goes in v1:
time: 1320 us
  waiting for transfers between devices  731 us (55%)
  blocking collectives  302 us (23%)
  matrix products  203 us (15%)
  local copies, waits for them, and re-layouts  67.5 us (5%)
  between operations  13.5 us (1%)
    all_gather x1, waiting for transfers between devices, local_mlp(): x_rows = lax.all_gather(x_full, 'dz', axis=0, tiled=True)  281 us
    all_gather x1, waiting for transfers between devices, local_mlp(): h_rows = lax.all_gather(hidden, 'dy', axis=1, tiled=True)  259 us
    all_to_all x1, blocking collectives, local_mlp(): wg = lax.all_to_all(wg_blk, 'dy', split_axis=1, concat_axis=0, tiled=True)  193 us
    reduce_scatter x1, waiting for transfers between devices, local_mlp(): out_sum = lax.psum_scatter(out_part, 'dz', scatter_dimension=0, tiled=True)  189 us
    all_to_all x1, blocking collectives, local_mlp(): wu = lax.all_to_all(wu_blk, 'dy', split_axis=1, concat_axis=0, tiled=True)  109 us
    dot_general x1, matrix products, local_mlp(): up = jnp.dot(x_rows, wu, preferred_element_type=jnp.float32)  68.5 us
    dot_general x1, matrix products, local_mlp(): out_part = jnp.dot(h_rows, wd_perm, preferred_element_type=jnp.float32)  67.3 us
    dot_general x1, matrix products, local_mlp(): gate = jnp.dot(x_rows, wg, preferred_element_type=jnp.float32)  67.1 us
  transfers between devices with their start and end apart: 7, of which 3 were waited for; matrix products, arithmetic and copies ran while one was open for 15% of the time, Pallas kernels for 0%

profile of v1, /device:TPU:97, one launch (start us, length us, event | category | flops | bytes accessed | tf_op | source)
XLA Modules:
  0.0 1321.4 jit_solution(12212700784465213987)
XLA Ops:
  6.6 0.7 all-gather.7.cloned.1.call-update
  7.3 0.1 all-gather.11.cloned.1.call-start
  7.4 12.8 copy.5
  20.2 193.3 %all_to_all.38 = bf16[1792,4,640]{0,2,1:T(8,128)(2,1)} all-to-all(bf16[1792,4,640]{0,2,1:T(8,128)(2,1)} %bitcast.20), channel_id=1, replica_groups=mesh['grp'=1,'dz'=4,'dy'=4,'dx'=2] {'dy'}, dimensions={1} | all-to-all | bytes 18350080 | tf_op jit(solution)/shard_map/all_to_all | solution.py:13
  213.5 12.7 copy.6
  226.3 0.1 all-gather.9.cloned.1.call-start
  226.4 0.7 all-gather.9.cloned.1.call-update
  227.1 0.1 all-gather.13.cloned.1.call-start
  227.2 12.8 copy.7
  240.0 108.8 %all_to_all.39 = bf16[1792,4,640]{0,2,1:T(8,128)(2,1)} all-to-all(bf16[1792,4,640]{0,2,1:T(8,128)(2,1)} %bitcast.21), channel_id=1, replica_groups=mesh['grp'=1,'dz'=4,'dy'=4,'dx'=2] {'dy'}, dimensions={1} | all-to-all | bytes 18350080 | tf_op jit(solution)/shard_map/all_to_all | solution.py:14
  348.7 12.8 copy.8
  361.6 0.1 all-gather.17.cloned.1.call-start
  361.7 0.6 all-gather.17.cloned.1.call-update
  362.3 0.1 all-gather.15.cloned.1.call-start
  362.4 280.7 %all-gather.9.cloned.1.call-done = bf16[3072,7168]{1,0:T(8,128)(2,1)} async-done(((bf16[768,7168]{1,0:T(8,128)(2,1)}), bf16[3072,7168]{1,0:T(8,128)(2,1)}) %all-gather.9.cloned.1.call-update) | async-done | bytes 44040208 | tf_op jit(solution)/shard_map/all_gather | solution.py:18
  643.1 67.1 %convolution_convert_fusion.1 = bf16[3072,1280]{1,0:T(8,128)(2,1)} fusion(bf16[3072,7168]{1,0:T(8,128)(2,1)} %all-gather.9.cloned.1.call-done, bf16[7168,1280]{1,0:T(8,128)(2,1)} %all-gather.11.cloned.1.call-done), kind=kOutput, calls=%fused_computation.8 | convolution fusion | flops 56375377920 | bytes 70254592 | tf_op jit(solution)/shard_map/dot_general | solution.py:19
  710.2 68.5 %fusion.4 = bf16[3072,1280]{1,0:T(8,128)(2,1)} fusion(bf16[3072,1280]{1,0:T(8,128)(2,1)} %convolution_convert_fusion.1, bf16[3072,7168]{1,0:T(8,128)(2,1)} %all-gather.9.cloned.1.call-done, bf16[7168,1280]{1,0:T(8,128)(2,1)} %all-gather.13.cloned.1.call-done), kind=kOutput, calls=%fused_computation.6 | convolution fusion | flops 56406835200 | bytes 78118912 | tf_op jit(solution)/shard_map/dot_general | solution.py:20
  778.7 0.1 all-gather.15.cloned.1.call-update
  778.7 0.1 reduce-scatter.2.cloned.1.call-start
  778.8 16.3 %copy.9 = bf16[4,2,640,1792]{3,2,1,0:T(8,128)(2,1)} copy(bf16[4,2,640,1792]{3,2,0,1:T(8,128)(2,1)} %bitcast.22) | data formatting | bytes 36700160 | tf_op jit(solution)/shard_map/transpose | solution.py:28
  795.2 258.7 %all-gather.15.cloned.1.call-done = bf16[3072,5120]{1,0:T(8,128)(2,1)} async-done(((bf16[3072,1280]{1,0:T(8,128)(2,1)}), bf16[3072,5120]{1,0:T(8,128)(2,1)}) %all-gather.15.cloned.1.call-update) | async-done | bytes 31457296 | tf_op jit(solution)/shard_map/all_gather | solution.py:25
  1053.9 67.3 %fusion.5 = f32[3072,1792]{1,0:T(8,128)} fusion(bf16[3072,5120]{1,0:T(8,128)(2,1)} %all-gather.15.cloned.1.call-done, bf16[5120,1792]{1,0:T(8,128)(2,1)} %bitcast.23), kind=kOutput, calls=%fused_computation.9 | convolution fusion | flops 56371445760 | bytes 71827456 | tf_op jit(solution)/shard_map/dot_general | solution.py:29
  1121.3 188.9 %reduce-scatter.2.cloned.1.call-done = f32[768,1792]{1,0:T(8,128)} async-done(((f32[3072,1792]{1,0:T(8,128)}), f32[768,1792]{1,0:T(8,128)}) %reduce-scatter.2.cloned.1.call-update) | async-done | bytes 5505040 | tf_op jit(solution)/shard_map/reduce_scatter | solution.py:30
  1310.1 4.4 convert_element_type.23
  (8 shorter events, 0.2 us)
Async XLA Ops:
  6.5 219.9 %all-gather.7.cloned.1.call-start = ((), (), s32[]{:S(2)}) async-start(), calls=%async_computation.3 | async-start | bytes 13762560 | tf_op jit(solution)/shard_map/all_gather | solution.py:17
  7.3 355.1 %all-gather.11.cloned.1.call-start = ((), (), s32[]{:S(2)}) async-start(), calls=%async_computation.5 | async-start | bytes 27525120 | tf_op jit(solution)/shard_map/all_gather | solution.py:15
  226.3 416.8 %all-gather.9.cloned.1.call-start = ((), (), s32[]{:S(2)}) async-start(), calls=%async_computation.4 | async-start | bytes 55050240 | tf_op jit(solution)/shard_map/all_gather | solution.py:18
  227.1 483.1 %all-gather.13.cloned.1.call-start = ((), (), s32[]{:S(2)}) async-start(), calls=%async_computation.6 | async-start | bytes 27525120 | tf_op jit(solution)/shard_map/all_gather | solution.py:16
  361.6 417.2 %all-gather.17.cloned.1.call-start = ((), (), s32[]{:S(2)}) async-start(), calls=%async_computation.8 | async-start | bytes 27525120 | tf_op jit(solution)/shard_map/all_gather | solution.py:26
  362.3 691.6 %all-gather.15.cloned.1.call-start = ((), (), s32[]{:S(2)}) async-start(), calls=%async_computation.7 | async-start | bytes 39321600 | tf_op jit(solution)/shard_map/all_gather | solution.py:25
  778.7 531.4 %reduce-scatter.2.cloned.1.call-start = ((), (), s32[]{:S(2)}) async-start(), calls=%async_computation.9 | async-start | bytes 27525120 | tf_op jit(solution)/shard_map/reduce_scatter | solution.py:30
Sparse Core Ops, SparseCore 0:
  8.9 203.7 all-gather.6
  226.5 35.4 all-gather.10
  263.5 379.5 all-gather.8
  644.5 35.1 all-gather.12
  681.2 35.0 all-gather.16
  778.9 275.0 all-gather.14
  1121.4 188.7 reduce-scatter.1

commit v2 on v0

v2 whole, which is shorter than its diff:
```python
import functools

import jax
import jax.numpy as jnp
from jax import lax
from jax.experimental import pallas as pl
from jax.experimental.pallas import tpu as pltpu
from jax.sharding import PartitionSpec as P

MESH = pl.DeviceIdType.MESH
RING = 4
H_SLOTS = 4
Z_SLOTS = 4
LAG = 2
XL, XS, XF, YL, YS, YF, WN, W2, WF, WL, SW, SD, P1 = 0, 2, 3, 5, 9, 13, 17, 19, 21, 23, 25, 33, 34


def _tile(extent, most):
    return next(t for t in range(most, 0, -128) if extent % t == 0)


def _kernel(mb, zb, x_in, wg_in, wu_in, wd_in, out, xg, wgu, ws, hg, wd, zin,
            xbuf, wbuf, hz, wdbuf, zinb, zout, ofin, hout,
            p1s, p1r, bin_s, bout_s, xsem, wsem, hzsem, wdsem, zinsem, osem,
            ols, olr, oss, osr, fs, fr, hws, zs, zr):
    rows, kb = x_in.shape
    hc = wg_in.shape[1] // RING
    nloc = wg_in.shape[1]
    hq = 2 * hc
    mc = wd_in.shape[1]
    tn = hout.shape[2]
    zn = zout.shape[2]
    nt = hq // tn
    nz = 2 * mc // zn
    ng = RING * nt
    zpi = -(-nz // (nt - 1))
    zstart = nt + 2

    b = lax.axis_index("dz")
    a = lax.axis_index("dy")
    c = lax.axis_index("dx")
    step = 1 - 2 * c
    al = lax.rem(a + step + RING, RING)
    ash = lax.rem(a - step + RING, RING)
    a2 = lax.rem(a + 2, RING)
    bl = lax.rem(b + step + RING, RING)
    bsh = lax.rem(b - step + RING, RING)
    xl, xs_ = {"dy": al}, {"dy": ash}
    yl, ys_ = {"dz": bl}, {"dz": bsh}
    sib = {"dx": 1 - c}
    kbs = (a, ash, al, a2)
    w_in = (wg_in, wu_in)

    def dest(s):
        return lax.rem(b - step * (1 + s) + 2 * RING, RING)

    def rc(src, dst, ss, rs, dev):
        return pltpu.make_async_remote_copy(src_ref=src, dst_ref=dst, send_sem=ss, recv_sem=rs, device_id=dev, device_id_type=MESH)

    def lanes(i, n):
        return pl.ds(pl.multiple_of(i * n, 128), n)

    def krows(k):
        return pl.ds(pl.multiple_of(k * kb, 16), kb)

    half = rows // 2

    def p1(i):
        sem = (p1s.at[i], p1r.at[i])
        if i < XS:
            r = pl.ds((i - XL) * half, half)
            return rc(x_in.at[r], xg.at[b, a, r], *sem, xl)
        if i < XF:
            return rc(x_in, xg.at[b, a], *sem, xs_)
        if i < YL:
            r = pl.ds((i - XF) * half, half)
            return rc(xg.at[b, ash, r], xg.at[b, ash, r], *sem, xl)
        if i < YF:
            j = (i - YL) % RING
            src = x_in if j == 0 else xg.at[b, kbs[j]]
            return rc(src, xg.at[b, kbs[j]], *sem, yl if i < YS else ys_)
        if i < WN:
            j = i - YF
            return rc(xg.at[bsh, kbs[j]], xg.at[bsh, kbs[j]], *sem, yl)
        if i < W2:
            u = i - WN
            return rc(w_in[u].at[:, lanes(ash, hc)], wgu.at[u, krows(a), lanes(c, hc)], *sem, xs_)
        if i < WF:
            u = i - W2
            return rc(w_in[u].at[:, lanes(a2, hc)], ws.at[u], *sem, xl)
        if i < WL:
            u = i - WF
            return rc(ws.at[u], wgu.at[u, krows(ash), lanes(c, hc)], *sem, xl)
        if i < SW:
            u = i - WL
            return rc(w_in[u].at[:, lanes(al, hc)], wgu.at[u, krows(a), lanes(c, hc)], *sem, xl)
        if i < SD:
            j, u = (i - SW) // 2, (i - SW) % 2
            dst = wgu.at[u, krows(kbs[j]), lanes(c, hc)]
            return rc(w_in[u].at[:, lanes(a, hc)] if j == 0 else dst, dst, *sem, sib)
        return rc(wd_in, wd.at[:, lanes(c, mc)], *sem, sib)

    def go(*idx):
        for i in idx:
            p1(i).start()

    def got(*idx):
        for i in idx:
            p1(i).wait_recv()

    barrier = pltpu.get_barrier_semaphore()
    for dev in (xl, xs_, yl, ys_, sib):
        pl.semaphore_signal(barrier, inc=1, device_id=dev, device_id_type=MESH)
    pl.semaphore_wait(barrier, 5)

    go(XL, XL + 1, XS, YL, YS, SD, SW, SW + 1, WN, WN + 1)

    moves = [(x_in, xg.at[b, a], xbuf.at[0, :, pl.ds(0, kb)])]
    col = kb
    for u in range(2):
        for r0 in range(0, kb, rows):
            n = min(rows, kb - r0)
            src = w_in[u].at[pl.ds(r0, n), lanes(a, hc)]
            dst = wgu.at[u, pl.ds(pl.multiple_of(a * kb + r0, 16), n), lanes(c, hc)]
            moves.append((src, dst, xbuf.at[0, pl.ds(0, n), pl.ds(col, hc)]))
            col += hc
    per = max(1, min(rows, wd_in.shape[0]))
    col = 0
    for r0 in range(0, wd_in.shape[0], per):
        n = min(per, wd_in.shape[0] - r0)
        moves.append((wd_in.at[pl.ds(r0, n)], wd.at[pl.ds(r0, n), lanes(c, mc)], xbuf.at[1, pl.ds(0, n), pl.ds(col, mc)]))
        col += mc
    for i, (src, _, mid) in enumerate(moves):
        pltpu.make_async_copy(src, mid, bin_s.at[i]).start()
    for i, (src, dst, mid) in enumerate(moves):
        pltpu.make_async_copy(src, mid, bin_s.at[i]).wait()
        pltpu.make_async_copy(mid, dst, bout_s.at[i]).start()
    zinb[...] = jnp.zeros_like(zinb)
    for i, (_, dst, mid) in enumerate(moves):
        pltpu.make_async_copy(mid, dst, bout_s.at[i]).wait()

    got(XL)
    go(XF)
    got(XL + 1)
    go(XF + 1, W2, W2 + 1, YL + 1)
    got(XS)
    go(YL + 2)
    got(YL)
    go(YF)
    got(XF, XF + 1)
    go(YL + 3, WL)
    got(YL + 1)
    go(YF + 1)
    got(W2)
    go(WF)
    got(W2 + 1)
    go(WF + 1, WL + 1)
    got(YL + 2)
    go(YF + 2)
    got(WN, WN + 1)
    go(SW + 4, SW + 5)
    got(YL + 3)
    go(YF + 3)
    got(YF, YF + 1)
    go(YS + 1)
    got(WL)
    go(SW + 2)
    got(WF)
    go(SW + 6)
    got(YF + 2)
    go(YS + 2)
    got(WF + 1)
    go(SW + 7)
    got(YF + 3)
    go(YS + 3)
    got(WL + 1)
    go(SW + 3)

    def x_load(s, k):
        return pltpu.make_async_copy(xg.at[dest(s), k], xbuf.at[lax.rem(s, 2), :, pl.ds(k * kb, kb)], xsem.at[lax.rem(s, 2), k])

    def w_load(g, u):
        slot = lax.rem(g, 2)
        return pltpu.make_async_copy(wgu.at[u, :, lanes(lax.rem(g, nt), tn)], wbuf.at[slot, :, pl.ds(u * tn, tn)], wsem.at[slot, u])

    def wd_load(z, i):
        slot, n = lax.rem(z, 2), lax.rem(z, nz)
        aa, cc = i // 2, i % 2
        src = wd.at[pl.ds(cc * nloc + aa * hc, hc), lanes(n, zn)]
        return pltpu.make_async_copy(src, wdbuf.at[slot, pl.ds(i * hc, hc)], wdsem.at[slot, i])

    def zin_load(z):
        return pltpu.make_async_copy(zin.at[z // nz - 1, lax.rem(z, nz)], zinb.at[lax.rem(z, 2)], zinsem.at[lax.rem(z, 2)])

    def h_write(g):
        slot = lax.rem(g, H_SLOTS)
        return pltpu.make_async_copy(hout.at[slot], hg.at[dest(g // nt), a, lax.rem(g, nt)], hws.at[slot])

    def h_long(g):
        slot = lax.rem(g, H_SLOTS)
        return rc(hout.at[slot], hg.at[dest(g // nt), a, lax.rem(g, nt)], ols.at[slot], olr.at[g], xl)

    def h_short(g):
        slot = lax.rem(g, H_SLOTS)
        return rc(hout.at[slot], hg.at[dest(g // nt), a, lax.rem(g, nt)], oss.at[slot], osr.at[g], xs_)

    def h_fwd(g):
        blk = hg.at[dest(g // nt), ash, lax.rem(g, nt)]
        return rc(blk, blk, fs.at[g], fr.at[g], xl)

    def z_send(z):
        slot = lax.rem(z, Z_SLOTS)
        return rc(zout.at[slot], zin.at[z // nz, lax.rem(z, nz)], zs.at[slot], zr.at[z], yl)

    def o_write(z):
        slot = lax.rem(z, 2)
        return pltpu.make_async_copy(ofin.at[slot], out.at[:, lanes(lax.rem(z, nz), zn)], osem.at[slot])

    def start_w(g):
        w_load(g, 0).start()
        w_load(g, 1).start()

    for k in range(RING):
        x_load(0, k).start()
    got(*range(SW, SD + 1))
    start_w(0)
    for i in range(8):
        wd_load(0, i).start()

    def z_tile(z, carry):
        s, slot = z // nz, lax.rem(z, 2)

        @pl.when(z + 1 < RING * nz)
        def _():
            for i in range(8):
                wd_load(z + 1, i).start()

        @pl.when((z + 1 >= nz) & (z + 1 < RING * nz))
        def _():
            z_send(z + 1 - nz).wait_recv()
            zin_load(z + 1).start()

        for i in range(8):
            wd_load(z, i).wait()

        @pl.when(s > 0)
        def _():
            zin_load(z).wait()

        @pl.when((z >= Z_SLOTS) & (z - Z_SLOTS < (RING - 1) * nz))
        def _():
            z_send(z - Z_SLOTS).wait_send()

        @pl.when(z - 2 >= (RING - 1) * nz)
        def _():
            o_write(z - 2).wait()

        zslot = lax.rem(z, Z_SLOTS)

        def part(m, carry):
            r = pl.ds(pl.multiple_of(m * zb, zb), zb)
            acc = jnp.dot(hz[r, :], wdbuf[slot], preferred_element_type=jnp.float32) + zinb[slot, r, :]
            zout[zslot, r, :] = acc
            ofin[slot, r, :] = acc.astype(jnp.bfloat16)
            return carry

        lax.fori_loop(0, rows // zb, part, 0)

        @pl.when(s < RING - 1)
        def _():
            z_send(z).start()

        @pl.when(s == RING - 1)
        def _():
            o_write(z).start()

        return carry

    def body(g, carry):
        s, t = g // nt, lax.rem(g, nt)

        @pl.when(g < ng)
        def _():
            @pl.when(g + 1 < ng)
            def _():
                start_w(g + 1)

            @pl.when((t == nt - 1) & (g + 1 < ng))
            def _():
                @pl.when(s + 1 == 2)
                def _():
                    got(*range(YS, YF))

                for k in range(RING):
                    x_load(s + 1, k).start()

            @pl.when(t == 0)
            def _():
                for k in range(RING):
                    x_load(s, k).wait()

            w_load(g, 0).wait()
            w_load(g, 1).wait()

            @pl.when(g >= H_SLOTS)
            def _():
                h_long(g - H_SLOTS).wait_send()
                h_short(g - H_SLOTS).wait_send()

            xslot, wslot, hslot = lax.rem(s, 2), lax.rem(g, 2), lax.rem(g, H_SLOTS)

            def part(m, carry):
                r = pl.ds(pl.multiple_of(m * mb, mb), mb)
                gu = jnp.dot(xbuf[xslot, r, :], wbuf[wslot], preferred_element_type=jnp.float32)
                gate = gu[:, :tn].astype(jnp.bfloat16).astype(jnp.float32)
                up = gu[:, tn:].astype(jnp.bfloat16).astype(jnp.float32)
                hout[hslot, r, :] = (jax.nn.silu(gate) * up).astype(jnp.bfloat16)
                return carry

            lax.fori_loop(0, rows // mb, part, 0)
            h_long(g).start()
            h_short(g).start()
            h_write(g).start()

        @pl.when((g >= 1) & (g <= ng))
        def _():
            h_write(g - 1).wait()

        q = jnp.maximum(g - zstart, 0)
        zs_, r_ = q // nt, lax.rem(q, nt)
        lo = jnp.where(g < zstart, 0, nz * zs_ + jnp.minimum(zpi * r_, nz))
        hi = jnp.where(g < zstart, 0, nz * zs_ + jnp.minimum(zpi * (r_ + 1), nz))

        @pl.when((g >= zstart) & (r_ == 0))
        def _():
            def arrived(j, carry):
                h_short(zs_ * nt + j).wait_recv()
                h_fwd(zs_ * nt + j).wait_recv()
                return carry

            lax.fori_loop(0, nt, arrived, 0)

            def piece(i):
                return pltpu.make_async_copy(hg.at[dest(zs_), i // nt, lax.rem(i, nt)], hz.at[:, lanes(i, tn)], hzsem.at[i])

            def fetch(i, carry):
                piece(i).start()
                return carry

            def fetched(i, carry):
                piece(i).wait()
                return carry

            lax.fori_loop(0, RING * nt, fetch, 0)
            lax.fori_loop(0, RING * nt, fetched, 0)

        lax.fori_loop(lo, hi, z_tile, 0)

        @pl.when((g >= LAG) & (g - LAG < ng))
        def _():
            h_long(g - LAG).wait_recv()
            h_fwd(g - LAG).start()

        return carry

    lax.fori_loop(0, zstart + (RING - 1) * nt + -(-nz // zpi), body, 0)

    for z in range(RING * nz - 2, RING * nz):
        o_write(z).wait()
    for i in range(P1):
        p1(i).wait_send()
    for g in range(ng - H_SLOTS, ng):
        h_long(g).wait_send()
        h_short(g).wait_send()

    def drain(g, carry):
        h_fwd(g).wait_send()
        return carry

    lax.fori_loop(0, ng, drain, 0)
    for z in range(max(0, RING * nz - Z_SLOTS), (RING - 1) * nz):
        z_send(z).wait_send()


def _local(x_blk, wg_blk, wu_blk, wd_blk):
    rows, kb = x_blk.shape
    hc = wg_blk.shape[1] // RING
    mc = wd_blk.shape[1]
    tn, zn = _tile(2 * hc, 256), _tile(2 * mc, 256)
    nt, nz = 2 * hc // tn, 2 * mc // zn
    n_moves = 1 + 2 * -(-kb // rows) + -(-wd_blk.shape[0] // rows)
    bf16, f32 = jnp.bfloat16, jnp.float32
    hbm = pl.BlockSpec(memory_space=pl.ANY)
    mb = rows // 2 if rows % 256 == 0 else rows
    zb = mb
    dma = pltpu.SemaphoreType.DMA
    flops = 2 * RING * rows * (RING * kb * 4 * hc + wd_blk.shape[0] * 2 * mc)
    res = pl.pallas_call(
        functools.partial(_kernel, mb, zb),
        name="ring_mlp",
        out_shape=(
            jax.ShapeDtypeStruct((rows, 2 * mc), bf16),
            jax.ShapeDtypeStruct((RING, RING, rows, kb), bf16),
            jax.ShapeDtypeStruct((2, RING * kb, 2 * hc), bf16),
            jax.ShapeDtypeStruct((2, kb, hc), bf16),
            jax.ShapeDtypeStruct((RING, RING, nt, rows, tn), bf16),
            jax.ShapeDtypeStruct((wd_blk.shape[0], 2 * mc), bf16),
            jax.ShapeDtypeStruct((RING - 1, nz, rows, zn), f32),
        ),
        in_specs=[hbm] * 4,
        out_specs=(hbm,) * 7,
        scratch_shapes=[
            pltpu.VMEM((2, rows, RING * kb), bf16),
            pltpu.VMEM((2, RING * kb, 2 * tn), bf16),
            pltpu.VMEM((rows, wd_blk.shape[0]), bf16),
            pltpu.VMEM((2, wd_blk.shape[0], zn), bf16),
            pltpu.VMEM((2, rows, zn), f32),
            pltpu.VMEM((Z_SLOTS, rows, zn), f32),
            pltpu.VMEM((2, rows, zn), bf16),
            pltpu.VMEM((H_SLOTS, rows, tn), bf16),
            dma((P1,)), dma((P1,)), dma((n_moves,)), dma((n_moves,)),
            dma((2, RING)), dma((2, 2)), dma((RING * nt,)), dma((2, 8)), dma((2,)), dma((2,)),
            dma((H_SLOTS,)), dma((RING * nt,)), dma((H_SLOTS,)), dma((RING * nt,)),
            dma((RING * nt,)), dma((RING * nt,)), dma((H_SLOTS,)),
            dma((Z_SLOTS,)), dma(((RING - 1) * nz,)),
        ],
        compiler_params=pltpu.CompilerParams(collective_id=0, has_side_effects=True, vmem_limit_bytes=67043328),
        cost_estimate=pl.CostEstimate(flops=flops, bytes_accessed=flops // 500, transcendentals=0),
    )(x_blk, wg_blk, wu_blk, wd_blk)
    return res[0]


def solution(mesh):
    assert mesh.shape["dz"] == RING and mesh.shape["dy"] == RING and mesh.shape["dx"] == 2
    x_spec = P(("grp", "dx", "dz"), "dy")
    w_in_spec = P("dy", ("dz", "dx"))
    w_out_spec = P("dz", ("dy", "dx"))
    return jax.shard_map(_local, mesh=mesh, in_specs=(x_spec, w_in_spec, w_in_spec, w_out_spec), out_specs=x_spec, check_vma=False)
```

time: 1830 us -> 661 us (0.36)
  waiting for transfers between devices: 1600 us -> 0 us
  Pallas kernels: 0 us -> 658 us
  matrix products: 200 us -> 0 us
  other arithmetic: 18.3 us -> 0 us
    reduce_scatter x3 -> x0, waiting for transfers between devices: 1160 us -> none  [the longest x1 519 us: local_mlp(): up_sum = lax.psum_scatter(up_part, 'dy', scatter_dimension=0, tiled=True)]
    pallas_call x0 -> x1, Pallas kernels: none -> 658 us  [_local(): pl.pallas_call(functools.partial(_kernel, mb, zb), name='ring_mlp', out_s...]
    all_gather x5 -> x0, waiting for transfers between devices: 441 us -> none  [the longest x1 277 us: local_mlp(): h_rows = lax.all_gather(hidden, 'dy', axis=0, tiled=True)]
    dot_general x3 -> x0, matrix products: 200 us -> none  [the longest x1 67.3 us: local_mlp(): out_part = jnp.dot(h_rows, wd_cols, preferred_element_type=jnp.float32)]
    convert_element_type x2 -> x0, other arithmetic: 18.3 us -> none  [the longest x1 13.9 us: local_mlp(): hidden = (jax.nn.silu(gate_val) * up_val).astype(jnp.bfloat16)]
  transfers between devices with their start and end apart: 8 -> 0, of which waited for: 7 -> 0; matrix products, arithmetic and copies ran while one was open for 8% -> 0% of each run, Pallas kernels for 0% -> 0%
where the time goes in v2:
time: 661 us
  Pallas kernels  658 us (100%)
    pallas_call x1, Pallas kernels, _local(): pl.pallas_call(functools.partial(_kernel, mb, zb), name='ring_mlp', out_s...  658 us

profile of v2, /device:TPU:97, one launch (start us, length us, event | category | flops | bytes accessed | tf_op | source)
XLA Modules:
  0.0 661.2 jit_solution(74346220708065614)
XLA Ops:
  0.0 657.7 %ring_mlp.1 = (bf16[768,1792]{1,0:T(8,128)(2,1)}, bf16[4,4,768,1792]{3,2,1,0:T(8,128)(2,1)}, bf16[2,7168,1280]{2,1,0:T(8,128)(2,1)}, bf16[2,1792,640]{2,1,0:T(8,...) custom-call(bf16[768,1792]{1,0:T(8,128)(2,1)} %x_in.1, ...), custom_call_target="tpu_custom_call" | custom-call | flops 169114337280 | bytes 338228672 | tf_op jit(solution)/shard_map/ring_mlp/pallas_call | solution.py:398
  657.7 3.5 copy.6
